TPU v7x, 256 devices: a whole 4x4x8 slice. The times are simulated.
256 devices in a mesh: chip: 8 (over y, core), board: 8 (over z), cuts: 4 (over x).
Axes of the slice: x: 4, y: 4, z: 8, core: 2. Of those that a mesh axis runs over, the one named last changes fastest.
Arguments:
- features: bfloat16 [256, 2048, 1024], P(('chip', 'board', 'cuts')), may hold values from -6 to 6
- targets: bfloat16 [256, 2048, 256], P(('chip', 'board', 'cuts')), may hold values from -24 to 24
- lower_weight: bfloat16 [256, 1024, 512], P(('chip', 'board', 'cuts')), may hold values from -0.1875 to 0.1875
- head_weight: float32 [256, 512, 256], P(('chip', 'board', 'cuts')), may hold values from -0.25 to 0.25
- batch_rows: int32 [256, 2, 1024], P(('chip', 'board', 'cuts')), may hold values from 0 to 2047
- sample_counts: int32 [256], P(('chip', 'board', 'cuts')), may hold values from 1 to 1000
- cluster_ids: int32 [256], P(('chip', 'board', 'cuts')), may hold values from 0 to 7, as said below
Outputs:
- cluster_step: float32 [256, 512, 256], P(('chip', 'board', 'cuts'))
Inputs may be any that keep to these rules, and one draw needn't show every extreme that they name: `cluster_ids`: every one of the 8 clusters has at least one client.
All inputs are finite; a program needn't handle non-finite values.
Results may differ from a plain program's by a relative error of at most 0.0003.
Values sent between devices are 32-bit elements; how exact they have to be, the bound alone decides.
A program may use at most 64 MiB of HBM per device.

v0:
```python
import jax
import jax.numpy as jnp
from jax import lax
from jax.sharding import Mesh
from jax.sharding import PartitionSpec as P

CHIP = ("chip_0", "chip_1")
CHIP_BOARD_CUTS = ("chip_0", "chip_1", "board", "cuts")


LR = 0.5


def laid_out(blocks, dim):
    blocks = jnp.moveaxis(blocks, 0, dim)
    dims = blocks.shape
    return blocks.reshape(*dims[:dim], dims[dim] * dims[dim + 1], *dims[dim + 2 :])


def gather_in_order(value, axes, order):
    blocks = value[None]
    for k in order:
        blocks = lax.all_gather(blocks, axes[k], axis=0, tiled=True)
    block = [lax.axis_size(axes[k]) for k in reversed(order)]
    blocks = blocks.reshape(*block, *value.shape)
    turned = sorted(range(len(order)), key=lambda place: order[len(order) - 1 - place])
    return blocks.transpose(*turned, *range(len(order), blocks.ndim)).reshape(-1, *value.shape)


def gathered_by_axis(value, axes, order, dim):
    return laid_out(gather_in_order(value, axes, order), dim)


def cut_along(value, dim, peers):
    dims = value.shape
    blocks = value.reshape(*dims[:dim], peers, dims[dim] // peers, *dims[dim + 1 :])
    return jnp.moveaxis(blocks, dim, 0)


def exchange_both(value, axis, axes, splits, concats):
    sizes = [lax.axis_size(a) for a in axes]
    blocks = cut_along(value, splits[0], sizes[0])
    blocks = jnp.moveaxis(cut_along(blocks, splits[1] + 1, sizes[1]), 0, 1)
    inside = blocks.shape[2:]
    blocks = blocks.reshape(-1, *inside)
    blocks = lax.all_to_all(blocks, axis, split_axis=0, concat_axis=0, tiled=True)
    blocks = laid_out(blocks.reshape(*sizes, *inside), concats[0] + 1)
    return laid_out(blocks, concats[1])


def on_device(features, targets, lower_weight, head_weight, batch_rows, sample_counts, cluster_ids):
    hidden = jnp.tanh(jnp.dot(features[0], lower_weight[0], preferred_element_type=jnp.float32))
    start = head_weight[0]
    weight = start
    count_rows = batch_rows.shape[2]
    for step in range(batch_rows.shape[1]):
        picked = jnp.take(hidden, batch_rows[0, step], axis=0)
        wanted = jnp.take(targets[0], batch_rows[0, step], axis=0).astype(jnp.float32)
        err = jnp.dot(picked, weight, precision=lax.Precision.HIGHEST) - wanted
        grad = jnp.dot(picked.T, err, precision=lax.Precision.HIGHEST) / count_rows
        weight = weight - LR * grad
    delta = weight - start
    cluster = cluster_ids[0]
    number = 8
    chip_count = lax.axis_size(CHIP)
    rest_count = lax.axis_size(("board", "cuts"))
    every_id, every_count = (
        gathered_by_axis(cluster_ids, CHIP_BOARD_CUTS, (0, 2, 3, 1), 0),
        gathered_by_axis(sample_counts, CHIP_BOARD_CUTS, (0, 2, 3, 1), 0),
    )
    table = (every_id[:, None] == jnp.arange(number, dtype=jnp.int32)[None, :]).astype(jnp.float32)
    weighted = table * every_count.astype(jnp.float32)[:, None]
    counts = jnp.sum(weighted, axis=0)
    scaled = (sample_counts[0].astype(jnp.float32) * delta).reshape(chip_count, rest_count, -1)
    columns = exchange_both(scaled, CHIP_BOARD_CUTS, (CHIP, ("board", "cuts")), (0, 1), (0, 1))
    columns = columns.reshape(chip_count * rest_count, -1)
    share = jnp.dot(table.T, columns, precision=lax.Precision.HIGHEST)
    outgoing = jnp.dot(table, share, precision=lax.Precision.HIGHEST)
    outgoing = outgoing.reshape(chip_count, rest_count, -1)
    arrived = exchange_both(outgoing, CHIP_BOARD_CUTS, (CHIP, ("board", "cuts")), (0, 1), (0, 1))
    mine = arrived.reshape(delta.shape)
    denom = lax.dynamic_index_in_dim(counts, cluster, 0, keepdims=False)
    return (mine / (LR * denom))[None]


def solution(mesh):
    finer = Mesh(
        mesh.devices.reshape(4, 2, mesh.shape["board"], mesh.shape["cuts"]),
        ("chip_0", "chip_1", "board", "cuts"),
    )
    return jax.shard_map(
        on_device,
        mesh=finer,
        in_specs=(
            P(CHIP_BOARD_CUTS, None, None),
            P(CHIP_BOARD_CUTS, None, None),
            P(CHIP_BOARD_CUTS, None, None),
            P(CHIP_BOARD_CUTS, None, None),
            P(CHIP_BOARD_CUTS, None, None),
            P(CHIP_BOARD_CUTS),
            P(CHIP_BOARD_CUTS),
        ),
        out_specs=P(CHIP_BOARD_CUTS, None, None),
        check_vma=False,
    )
```

profile of v0, /device:TPU:1, one launch (start us, length us, event | category | flops | bytes accessed | tf_op | source)
XLA Modules:
  0.0 134.0 jit_solution(15748211880293948014)
XLA Ops:
  0.0 0.0 copy-start
  0.0 0.8 fusion.56
  0.9 0.4 copy-done
  1.3 6.5 %fusion.2 = f32[2048,512]{1,0:T(8,128)} fusion(bf16[1,2048,1024]{2,1,0:T(8,128)(2,1)} %param.11, bf16[1,1024,512]{2,1,0:T(8,128)(2,1)S(1)} %copy-done), kind=kOutput, calls=%fused_computation.6 | convolution fusion | flops 2147483648 | bytes 9437184 | tf_op jit(solution)/shard_map/dot_general | solution.py:52
  7.7 0.0 copy-start.1
  7.7 7.6 %gather_fusion = f32[1024,512]{1,0:T(8,128)} fusion(f32[2048,512]{1,0:T(8,128)} %fusion.2, s32[1024]{0:T(1024)S(1)} %fusion.50), kind=kCustom, calls=%fused_computation.clone | custom fusion | bytes 4198400 | tf_op jit(solution)/shard_map/jit(_take)/gather | solution.py:57
  15.3 0.0 copy-done.1
  15.3 5.0 %gather_fusion.1 = bf16[1024,256]{1,0:T(8,128)(2,1)} fusion(bf16[2048,256]{1,0:T(8,128)(2,1)S(1)} %bitcast.64, s32[1024]{0:T(1024)S(1)} %fusion.50), kind=kCustom, calls=%fused_computation.1.clone | custom fusion | bytes 1052672 | tf_op jit(solution)/shard_map/jit(_take)/gather | solution.py:58
  20.3 7.5 %gather_fusion.2 = f32[1024,512]{1,0:T(8,128)} fusion(f32[2048,512]{1,0:T(8,128)} %fusion.2, s32[1024]{0:T(1024)S(1)} %fusion.51), kind=kCustom, calls=%fused_computation.2.clone | custom fusion | bytes 4198400 | tf_op jit(solution)/shard_map/jit(_take)/gather | solution.py:57
  27.8 0.0 copy-start.4
  27.8 3.9 %gather_fusion.3 = bf16[1024,256]{1,0:T(8,128)(2,1)S(1)} fusion(bf16[2048,256]{1,0:T(8,128)(2,1)S(1)} %bitcast.65, s32[1024]{0:T(1024)S(1)} %fusion.51), kind=kCustom, calls=%fused_computation.3.clone | custom fusion | bytes 1052672 | tf_op jit(solution)/shard_map/jit(_take)/gather | solution.py:58
  31.7 0.0 copy-done.4
  31.7 0.0 copy-start.2
  31.7 3.7 %fusion.13 = f32[1024,256]{1,0:T(8,128)S(1)} fusion(f32[1024,512]{1,0:T(8,128)} %gather_fusion, pred[1024]{0:T(1024)(128)(4,1)S(1)} %compare_and_fusion.1, f32[1,512,256]{2,1,0:T(8,128)S(1)} %copy-done.4, bf16[1024,256]{1,0:T(8,128)(2,1)} %gather_fusion.1), kind=kOutput, calls=%fused_computation.15 | convolution fusion | flops 1611923456 | bytes 4195328 | tf_op jit(solution)/shard_map/dot_general | solution.py:59
  35.4 0.0 copy-done.2
  35.4 0.0 copy-start.3
  35.4 3.6 %fusion.34 = f32[512,256]{1,0:T(8,128)S(1)} fusion(f32[1024,256]{1,0:T(8,128)S(1)} %fusion.13, f32[1024,512]{1,0:T(8,128)S(1)} %copy-done.2, pred[1024]{0:T(1024)(128)(4,1)S(1)} %compare_and_fusion.1, f32[1,512,256]{2,1,0:T(8,128)S(1)} %copy-done.4), kind=kOutput, calls=%fused_computation.23 | convolution fusion | flops 1611399168 | bytes 4195328 | tf_op jit(solution)/shard_map/dot_general | solution.py:60
  39.7 0.0 copy-done.3
  39.7 2.6 %fusion.16 = f32[1024,256]{1,0:T(8,128)S(1)} fusion(f32[512,256]{1,0:T(8,128)S(1)} %fusion.34, f32[1024,512]{1,0:T(8,128)S(1)} %copy-done.3, pred[1024]{0:T(1024)(128)(4,1)S(1)} %compare_and_fusion, bf16[1024,256]{1,0:T(8,128)(2,1)S(1)} %gather_fusion.3), kind=kOutput, calls=%fused_computation.16 | convolution fusion | flops 1611923456 | bytes 4195328 | tf_op jit(solution)/shard_map/dot_general | solution.py:59
  42.3 3.6 %fusion.31 = f32[512,256]{1,0:T(8,128)S(1)} fusion(f32[512,256]{1,0:T(8,128)S(1)} %fusion.34, f32[1024,256]{1,0:T(8,128)S(1)} %fusion.16, f32[1024,512]{1,0:T(8,128)S(1)} %copy-done.3, pred[1024]{0:T(1024)(128)(4,1)S(1)} %compare_and_fusion, f32[1,512,256]{2,1,0:T(8,128)S(1)} %copy-done.4, f32[]{:T(128)} %bitcast.5), kind=kOutput, calls=%fused_computation.22 | convolution fusion | flops 1611661312 | bytes 4719620 | tf_op jit(solution)/shard_map/dot_general | solution.py:60
  46.0 0.0 copy-start.7
  46.0 0.0 copy-start.6
  46.0 0.0 copy-start.5
  46.0 1.3 reshape_transpose_transpose_reshape_reshape_reshape.8
  47.3 15.6 %all-to-all-start = ((f32[256,1,1,512]{3,2,1,0:T(1,128)}), f32[256,1,1,512]{3,2,1,0:T(1,128)S(1)}, u32[]{:S(2)}, u32[]{:S(2)}) async-start(f32[256,1,1,512]{3,2,1,0:T(1,128)} %reshape_transpose_transpose_reshape_reshape_reshape.8), calls=%async_computation | async-start | bytes 1048576 | tf_op jit(solution)/shard_map/all_to_all | solution.py:46
  63.6 0.0 copy-done.7
  63.6 0.6 dynamic-slice
  64.2 0.7 dynamic-update-slice.3
  64.9 0.7 dynamic-update-slice
  65.6 7.6 %all-reduce.8 = (s32[4]{0:T(128)S(1)}, s32[4]{0:T(128)S(1)}) all-reduce(s32[4]{0:T(128)S(1)} %dynamic-update-slice, s32[4]{0:T(128)S(1)} %dynamic-update-slice.3), channel_id=2, replica_groups=mesh['chip_0'=4,'chip_1'=2,'board'=8,'cuts'=4] {'chip_0'}, use_global_device_ids=true, to_apply=%add | all-reduce | flops 8 | bytes 64
  73.2 0.0 copy-done.6
  73.2 0.6 dynamic-slice.1
  73.8 0.0 copy-done.5
  73.8 0.6 dynamic-slice.2
  75.0 0.2 dynamic-update-slice.1
  75.3 0.2 dynamic-update-slice.4
  76.1 12.4 %all-reduce.6 = (s32[32]{0:T(128)S(1)}, s32[32]{0:T(128)S(1)}) all-reduce(s32[32]{0:T(128)S(1)} %dynamic-update-slice.1, s32[32]{0:T(128)S(1)} %dynamic-update-slice.4), channel_id=3, replica_groups=mesh['chip_0'=4,'chip_1'=2,'board'=8,'cuts'=4] {'board'}, use_global_device_ids=true, to_apply=%add.1 | all-reduce | flops 64 | bytes 512
  88.4 0.2 dynamic-update-slice.2
  88.6 0.2 dynamic-update-slice.5
  88.8 6.9 %all-reduce.7 = (s32[128]{0:T(128)S(1)}, s32[128]{0:T(128)S(1)}) all-reduce(s32[128]{0:T(128)S(1)} %dynamic-update-slice.2, s32[128]{0:T(128)S(1)} %dynamic-update-slice.5), channel_id=4, replica_groups=mesh['chip_0'=4,'chip_1'=2,'board'=8,'cuts'=4] {'cuts'}, use_global_device_ids=true, to_apply=%add.2 | all-reduce | flops 256 | bytes 2048
  95.7 7.9 %all-gather.8 = s32[2,1,128]{2,1,0:T(1,128)S(1)} all-gather(s32[1,1,128]{2,1,0:T(1,128)S(1)} %bitcast.77), channel_id=5, replica_groups=mesh['chip_0'=4,'chip_1'=2,'board'=8,'cuts'=4] {'chip_1'}, dimensions={0}, use_global_device_ids=true | all-gather | bytes 1536 | tf_op jit(solution)/shard_map/all_gather | solution.py:23
  103.5 0.5 broadcast.59
  104.1 0.6 reduce.7
  104.6 0.1 reshape.49
  104.7 0.2 copy.14
  104.9 0.1 eq.15
  105.1 0.0 all-to-all-done
  105.1 0.3 fusion.47
  105.4 0.4 convolution_bitcast_fusion
  105.8 1.3 copy.16
  107.2 5.5 %all-to-all-start.1 = ((f32[256,1,1,512]{3,2,1,0:T(1,128)}), f32[256,1,1,512]{3,2,1,0:T(1,128)S(1)}, u32[]{:S(2)}, u32[]{:S(2)}) async-start(f32[256,1,1,512]{3,2,1,0:T(1,128)} %copy.16), calls=%async_computation.1 | async-start | bytes 1048576 | tf_op jit(solution)/shard_map/all_to_all | solution.py:46
  112.7 3.6 %all-gather.9 = s32[2,1,128]{2,1,0:T(1,128)S(1)} all-gather(s32[1,1,128]{2,1,0:T(1,128)S(1)} %bitcast.76), channel_id=9, replica_groups=mesh['chip_0'=4,'chip_1'=2,'board'=8,'cuts'=4] {'chip_1'}, dimensions={0}, use_global_device_ids=true | all-gather | bytes 1536 | tf_op jit(solution)/shard_map/all_gather | solution.py:23
  116.3 0.1 convert_element_type.34
  116.4 0.2 copy.17
  116.6 0.1 convert_element_type.36
  116.8 0.1 select_reduce_fusion
  116.9 0.7 dynamic_slice.4
  118.2 14.5 %all-to-all-done.1 = f32[256,1,1,512]{3,2,1,0:T(1,128)S(1)} async-done(((f32[256,1,1,512]{3,2,1,0:T(1,128)}), f32[256,1,1,512]{3,2,1,0:T(1,128)S(1)}, u32[]{:S(2)}, u32[]{:S(2)}) %all-to-all-start.1) | async-done | bytes 524320 | tf_op jit(solution)/shard_map/all_to_all | solution.py:46
  132.7 0.4 broadcast_divide_fusion
  133.1 0.9 div.32
  (13 shorter events, 0.1 us)
Async XLA Ops:
  0.0 1.3 copy-start
  7.7 7.6 %copy-start.1 = (bf16[1,2048,256]{2,1,0:T(8,128)(2,1)S(1)}, bf16[1,2048,256]{2,1,0:T(8,128)(2,1)}, u32[]{:S(2)}) copy-start(bf16[1,2048,256]{2,1,0:T(8,128)(2,1)} %param.12) | copy-start | bytes 3145732
  27.8 3.9 %copy-start.4 = (f32[1,512,256]{2,1,0:T(8,128)S(1)}, f32[1,512,256]{2,1,0:T(8,128)}, u32[]{:S(2)}) copy-start(f32[1,512,256]{2,1,0:T(8,128)} %param.14) | copy-start | bytes 1572868
  31.7 3.7 %copy-start.2 = (f32[1024,512]{1,0:T(8,128)S(1)}, f32[1024,512]{1,0:T(8,128)}, u32[]{:S(2)}) copy-start(f32[1024,512]{1,0:T(8,128)} %gather_fusion) | copy-start | bytes 6291460
  35.4 4.3 %copy-start.3 = (f32[1024,512]{1,0:T(8,128)S(1)}, f32[1024,512]{1,0:T(8,128)}, u32[]{:S(2)}) copy-start(f32[1024,512]{1,0:T(8,128)} %gather_fusion.2) | copy-start | bytes 6291460
  46.0 17.7 %copy-start.7 = (u32[256]{0:T(256)S(1)}, u32[256]{0:T(256)}, u32[]{:S(2)}) copy-start(u32[256]{0:T(256)} %constant.48) | copy-start | bytes 3076
  46.0 27.2 %copy-start.6 = (u32[256]{0:T(256)S(1)}, u32[256]{0:T(256)}, u32[]{:S(2)}) copy-start(u32[256]{0:T(256)} %constant.53) | copy-start | bytes 3076
  46.0 27.8 %copy-start.5 = (u32[256]{0:T(256)S(1)}, u32[256]{0:T(256)}, u32[]{:S(2)}) copy-start(u32[256]{0:T(256)} %constant.58) | copy-start | bytes 3076
  47.3 57.7 %all-to-all-start = ((f32[256,1,1,512]{3,2,1,0:T(1,128)}), f32[256,1,1,512]{3,2,1,0:T(1,128)S(1)}, u32[]{:S(2)}, u32[]{:S(2)}) async-start(f32[256,1,1,512]{3,2,1,0:T(1,128)} %reshape_transpose_transpose_reshape_reshape_reshape.8), calls=%async_computation | async-start | bytes 1048576 | tf_op jit(solution)/shard_map/all_to_all | solution.py:46
  107.2 25.6 %all-to-all-start.1 = ((f32[256,1,1,512]{3,2,1,0:T(1,128)}), f32[256,1,1,512]{3,2,1,0:T(1,128)S(1)}, u32[]{:S(2)}, u32[]{:S(2)}) async-start(f32[256,1,1,512]{3,2,1,0:T(1,128)} %copy.16), calls=%async_computation.1 | async-start | bytes 1048576 | tf_op jit(solution)/shard_map/all_to_all | solution.py:46
where the time goes:
time: 134 us
  blocking collectives  38.4 us (29%)
  local copies, waits for them, and re-layouts  34.8 us (26%)
  starting transfers between devices  21.1 us (16%)
  matrix products  20.7 us (15%)
  waiting for transfers between devices  14.5 us (11%)
  between operations  3.45 us (3%)
    unnamed x3, blocking collectives  26.9 us
    all_to_all x2, starting transfers between devices, exchange_both(): lax.all_to_all(blocks, axis, split_axis=0, concat_axis=0, tiled=True)  21.1 us
    gather x2, local copies, waits for them, and re-layouts, on_device(): picked = jnp.take(hidden, batch_rows[0, step], axis=0)  15.1 us
    all_to_all x2, waiting for transfers between devices, exchange_both(): lax.all_to_all(blocks, axis, split_axis=0, concat_axis=0, tiled=True)  14.5 us
    all_gather x2, blocking collectives, gather_in_order(): blocks = lax.all_gather(blocks, axes[k], axis=0, tiled=True)  11.5 us
    gather x2, local copies, waits for them, and re-layouts, on_device(): jnp.take(targets[0], batch_rows[0, step], axis=0).astype(jnp.float32)  8.91 us
    dot_general x2, matrix products, on_device(): grad = jnp.dot(picked.T, err, precision=lax.Precision.HIGHEST) / count_rows  7.28 us
    dot_general x1, matrix products, on_device(): jnp.dot(features[0], lower_weight[0], preferred_element_type=jnp.float32)  6.45 us
  transfers between devices with their start and end apart: 2, of which 1 were waited for; matrix products, arithmetic and copies ran while one was open for 5% of the time, Pallas kernels for 0%

commit v1 on v0

--- a/solution.py
+++ b/solution.py
@@ -1,6 +1,9 @@
+import functools
 import jax
 import jax.numpy as jnp
 from jax import lax
+from jax.experimental import pallas as pl
+from jax.experimental.pallas import tpu as pltpu
 from jax.sharding import Mesh
 from jax.sharding import PartitionSpec as P
 
@@ -48,18 +51,87 @@
     return laid_out(blocks, concats[1])
 
 
+NB=4
+
+def split(v):
+    hi = v.astype(jnp.bfloat16)
+    lo = (v - hi.astype(jnp.float32)).astype(jnp.bfloat16)
+    return hi, lo
+
+NT=(((1,),(1,)),((),()))
+TN=(((0,),(0,)),((),()))
+def dg(a,b,d): return lax.dot_general(a,b,d,preferred_element_type=jnp.float32)
+
+def compute(feat, targ, low, head, rows, fv, tv, lv, hv, hh, hl, cm, sems, nb=NB):
+    pool = fv.shape[0]; blk = pool//nb
+    cps=[pltpu.make_async_copy(low.at[0], lv, sems.at[0])]
+    for b in range(nb):
+        cps.append(pltpu.make_async_copy(feat.at[0,pl.ds(b*blk,blk)], fv.at[pl.ds(b*blk,blk)], sems.at[1+b]))
+    ch=pltpu.make_async_copy(head.at[0], hv, sems.at[1+nb])
+    ct=pltpu.make_async_copy(targ.at[0], tv, sems.at[2+nb])
+    cps[0].start(); cps[1].start(); ch.start(); ct.start()
+    for c in cps[2:]: c.start()
+    count_rows = rows.shape[2]
+    for s in range(2):
+        idx = rows[0, pl.ds(s,1), :]
+        lowi = idx % 128
+        higi = idx // 128
+        bt = (lax.broadcasted_iota(jnp.int32,(128,count_rows),0)==lowi).astype(jnp.float32).astype(jnp.bfloat16)
+        at = (lax.broadcasted_iota(jnp.int32,(16,count_rows),0)==higi).astype(jnp.float32).astype(jnp.bfloat16)
+        cm[s] = dg(bt, at, NT)
+    cps[0].wait()
+    ch.wait(); ct.wait()
+    def err_scaled(s, b, hhb, hlb, wh, wl):
+        e = dg(hhb,wh,NT)+dg(hlb,wh,NT)+dg(hhb,wl,NT) - tv[pl.ds(b*blk,blk)].astype(jnp.float32)
+        per = blk//128
+        parts=[]
+        for q in range(per):
+            col = cm[s,:,pl.ds(b*per+q,1)]
+            parts.append(e[q*128:(q+1)*128]*col)
+        e = jnp.concatenate(parts,0) if per>1 else parts[0]
+        return split(e)
+    def grad_t(eh, el, hhb, hlb):
+        return dg(eh,hhb,TN)+dg(eh,hlb,TN)+dg(el,hhb,TN)
+    w0t = hv[...].T
+    wh,wl = split(w0t)
+    g = None
+    for b in range(nb):
+        cps[1+b].wait()
+        sl=pl.ds(b*blk,blk)
+        h = jnp.tanh(jnp.dot(fv[sl], lv[...], preferred_element_type=jnp.float32))
+        hhb,hlb = split(h)
+        hh[sl]=hhb; hl[sl]=hlb
+        eh,el = err_scaled(0,b,hhb,hlb,wh,wl)
+        t = grad_t(eh,el,hhb,hlb)
+        g = t if g is None else g+t
+    k = LR/count_rows
+    d1 = g*(-k)
+    wh,wl = split(w0t+d1)
+    g=None
+    for b in range(nb):
+        sl=pl.ds(b*blk,blk)
+        eh,el = err_scaled(1,b,hh[sl],hl[sl],wh,wl)
+        t = grad_t(eh,el,hh[sl],hl[sl])
+        g = t if g is None else g+t
+    return (d1 + g*(-k)).T
+
+def scratch(nb=NB):
+    return [pltpu.VMEM((2048,1024),jnp.bfloat16), pltpu.VMEM((2048,256),jnp.bfloat16), pltpu.VMEM((1024,512),jnp.bfloat16),
+            pltpu.VMEM((512,256),jnp.float32), pltpu.VMEM((2048,512),jnp.bfloat16), pltpu.VMEM((2048,512),jnp.bfloat16),
+            pltpu.VMEM((2,128,16),jnp.float32), pltpu.SemaphoreType.DMA((3+nb,))]
+
+def kern(feat,targ,low,head,rows,out,*scr, nb=NB):
+    out[...] = compute(feat,targ,low,head,rows,*scr,nb=nb)
+
+def local(feat,targ,low,head,rows,nb=NB):
+    A=pl.BlockSpec(memory_space=pl.ANY); V=pl.BlockSpec(memory_space=pltpu.VMEM)
+    return pl.pallas_call(functools.partial(kern,nb=nb), out_shape=jax.ShapeDtypeStruct((512,256),jnp.float32),
+        in_specs=[A,A,A,A,V], out_specs=V, scratch_shapes=scratch(nb),
+        compiler_params=pltpu.CompilerParams(vmem_limit_bytes=48*2**20))(feat,targ,low,head,rows)
+
+
 def on_device(features, targets, lower_weight, head_weight, batch_rows, sample_counts, cluster_ids):
-    hidden = jnp.tanh(jnp.dot(features[0], lower_weight[0], preferred_element_type=jnp.float32))
-    start = head_weight[0]
-    weight = start
-    count_rows = batch_rows.shape[2]
-    for step in range(batch_rows.shape[1]):
-        picked = jnp.take(hidden, batch_rows[0, step], axis=0)
-        wanted = jnp.take(targets[0], batch_rows[0, step], axis=0).astype(jnp.float32)
-        err = jnp.dot(picked, weight, precision=lax.Precision.HIGHEST) - wanted
-        grad = jnp.dot(picked.T, err, precision=lax.Precision.HIGHEST) / count_rows
-        weight = weight - LR * grad
-    delta = weight - start
+    delta = local(features, targets, lower_weight, head_weight, batch_rows)
     cluster = cluster_ids[0]
     number = 8
     chip_count = lax.axis_size(CHIP)

time: 134 us -> 108 us (0.81)
  local copies, waits for them, and re-layouts: 34.8 us -> 13.8 us
  matrix products: 20.7 us -> 0.71 us
  Pallas kernels: 0 us -> 14.9 us
    gather x4 -> x0, local copies, waits for them, and re-layouts: 24 us -> none  [the longest x2 15.1 us: on_device(): picked = jnp.take(hidden, batch_rows[0, step], axis=0)]
    dot_general x5 -> x0, matrix products: 20 us -> none  [the longest x2 7.28 us: on_device(): grad = jnp.dot(picked.T, err, precision=lax.Precision.HIGHEST) / count_rows]
    pallas_call x0 -> x1, Pallas kernels: none -> 14.9 us  [local(): pl.pallas_call(functools.partial(kern, nb=nb), out_shape=jax.ShapeDtypeSt...]
    unnamed x33 -> x31, local copies, waits for them, and re-layouts: 4.44 us -> 8.22 us
  transfers between devices with their start and end apart: 2 -> 2, of which waited for: 1 -> 1; matrix products, arithmetic and copies ran while one was open for 5% -> 6% of each run, Pallas kernels for 0% -> 0%
where the time goes in v1:
time: 108 us
  blocking collectives  38.4 us (36%)
  starting transfers between devices  21.1 us (20%)
  Pallas kernels  14.9 us (14%)
  waiting for transfers between devices  14.5 us (13%)
  local copies, waits for them, and re-layouts  13.8 us (13%)
  between operations  3.34 us (3%)
  other arithmetic  1.11 us (1%)
    unnamed x3, blocking collectives  26.8 us
    all_to_all x2, starting transfers between devices, exchange_both(): lax.all_to_all(blocks, axis, split_axis=0, concat_axis=0, tiled=True)  21.1 us
    pallas_call x1, Pallas kernels, local(): pl.pallas_call(functools.partial(kern, nb=nb), out_shape=jax.ShapeDtypeSt...  14.9 us
    all_to_all x2, waiting for transfers between devices, exchange_both(): lax.all_to_all(blocks, axis, split_axis=0, concat_axis=0, tiled=True)  14.5 us
    all_gather x2, blocking collectives, gather_in_order(): blocks = lax.all_gather(blocks, axes[k], axis=0, tiled=True)  11.5 us
    unnamed x31, local copies, waits for them, and re-layouts  8.22 us
    another operation x2, local copies, waits for them, and re-layouts, exchange_both(): blocks = blocks.reshape(-1, *inside)  2.66 us
  transfers between devices with their start and end apart: 2, of which 1 were waited for; matrix products, arithmetic and copies ran while one was open for 6% of the time, Pallas kernels for 0%

profile of v1, /device:TPU:1, one launch (start us, length us, event | category | flops | bytes accessed | tf_op | source)
XLA Modules:
  0.0 107.8 jit_solution(6438596653625524359)
XLA Ops:
  0.7 0.0 copy-start
  0.7 1.2 %copy-done = bf16[1,2048,256]{2,1,0:T(8,128)(2,1)S(1)} copy-done((bf16[1,2048,256]{2,1,0:T(8,128)(2,1)S(1)}, bf16[1,2048,256]{2,1,0:T(8,128)(2,1)}, u32[]{:S(2)}) %copy-start) | copy-done | bytes 1048600
  1.9 0.0 copy-start.1
  1.9 1.2 %copy-done.1 = bf16[1,1024,512]{2,1,0:T(8,128)(2,1)S(1)} copy-done((bf16[1,1024,512]{2,1,0:T(8,128)(2,1)S(1)}, bf16[1,1024,512]{2,1,0:T(8,128)(2,1)}, u32[]{:S(2)}) %copy-start.1) | copy-done | bytes 1048600
  3.1 0.0 copy-start.2
  3.1 1.0 copy-done.2
  4.1 0.0 copy-start.3
  4.1 0.7 copy-done.3
  4.8 0.0 copy-start.6
  4.8 0.0 copy-start.5
  4.8 0.0 copy-start.4
  4.8 14.9 %shard_map.73 = f32[512,256]{1,0:T(8,128)S(1)} custom-call(bf16[1,2048,1024]{2,1,0:T(8,128)(2,1)} %feat.1, bf16[1,2048,256]{2,1,0:T(8,128)(2,1)S(1)} %copy-done, bf16[1,1024,512]{2,1,0:T(8,128)(2,1)S(1)} %copy-done.1, f32[1,512,256]{2,1,0:T(8,128)S(1)} %copy-done.2, s32[1,2,1024]{2,1,0:T(2,128)S(1)} %copy-done.3), custom_call_target="tpu_custom_call" | custom-call | tf_op jit(solution)/shard_map/pallas_call | solution.py:128
  19.8 1.3 %reshape_transpose_transpose_reshape_reshape_reshape.8 = f32[256,1,1,512]{3,2,1,0:T(1,128)} reshape(f32[512,256]{1,0:T(8,128)S(1)} %broadcast_multiply_fusion) | data formatting | bytes 1048576 | tf_op jit(solution)/shard_map/reshape;transpose;transpose;reshape;reshape;reshape | solution.py:48
  21.1 15.6 %all-to-all-start = ((f32[256,1,1,512]{3,2,1,0:T(1,128)}), f32[256,1,1,512]{3,2,1,0:T(1,128)S(1)}, u32[]{:S(2)}, u32[]{:S(2)}) async-start(f32[256,1,1,512]{3,2,1,0:T(1,128)} %reshape_transpose_transpose_reshape_reshape_reshape.8), calls=%async_computation | async-start | bytes 1048576 | tf_op jit(solution)/shard_map/all_to_all | solution.py:49
  37.4 0.0 copy-done.6
  37.5 0.6 dynamic-slice
  38.0 0.7 dynamic-update-slice.3
  38.7 0.7 dynamic-update-slice
  39.4 7.6 %all-reduce.8 = (s32[4]{0:T(128)S(1)}, s32[4]{0:T(128)S(1)}) all-reduce(s32[4]{0:T(128)S(1)} %dynamic-update-slice, s32[4]{0:T(128)S(1)} %dynamic-update-slice.3), channel_id=2, replica_groups=mesh['chip_0'=4,'chip_1'=2,'board'=8,'cuts'=4] {'chip_0'}, use_global_device_ids=true, to_apply=%add | all-reduce | flops 8 | bytes 64
  47.0 0.0 copy-done.5
  47.0 0.6 dynamic-slice.2
  47.6 0.0 copy-done.4
  47.6 0.6 dynamic-slice.1
  49.4 0.2 dynamic-update-slice.1
  49.6 0.2 dynamic-update-slice.4
  49.9 12.3 %all-reduce.6 = (s32[32]{0:T(128)S(1)}, s32[32]{0:T(128)S(1)}) all-reduce(s32[32]{0:T(128)S(1)} %dynamic-update-slice.1, s32[32]{0:T(128)S(1)} %dynamic-update-slice.4), channel_id=3, replica_groups=mesh['chip_0'=4,'chip_1'=2,'board'=8,'cuts'=4] {'board'}, use_global_device_ids=true, to_apply=%add.1 | all-reduce | flops 64 | bytes 512
  62.2 0.2 dynamic-update-slice.2
  62.4 0.2 dynamic-update-slice.5
  62.6 6.9 %all-reduce.7 = (s32[128]{0:T(128)S(1)}, s32[128]{0:T(128)S(1)}) all-reduce(s32[128]{0:T(128)S(1)} %dynamic-update-slice.2, s32[128]{0:T(128)S(1)} %dynamic-update-slice.5), channel_id=4, replica_groups=mesh['chip_0'=4,'chip_1'=2,'board'=8,'cuts'=4] {'cuts'}, use_global_device_ids=true, to_apply=%add.2 | all-reduce | flops 256 | bytes 2048
  69.5 7.9 %all-gather.8 = s32[2,1,128]{2,1,0:T(1,128)S(1)} all-gather(s32[1,1,128]{2,1,0:T(1,128)S(1)} %bitcast.52), channel_id=5, replica_groups=mesh['chip_0'=4,'chip_1'=2,'board'=8,'cuts'=4] {'chip_1'}, dimensions={0}, use_global_device_ids=true | all-gather | bytes 1536 | tf_op jit(solution)/shard_map/all_gather | solution.py:26
  77.3 0.5 broadcast.35
  77.8 0.6 reduce.7
  78.4 0.1 reshape.39
  78.5 0.2 copy.14
  78.7 0.1 eq.15
  78.9 0.0 all-to-all-done
  78.9 0.3 fusion
  79.2 0.4 convolution_bitcast_fusion
  79.6 1.3 %copy.16 = f32[256,1,1,512]{3,2,1,0:T(1,128)} copy(f32[256,1,1,512]{3,0,2,1:T(8,128)S(1)} %convolution_bitcast_fusion) | data formatting | bytes 1048576 | tf_op jit(solution)/shard_map/reshape;transpose;transpose;reshape;reshape;reshape | solution.py:48
  81.0 5.5 %all-to-all-start.1 = ((f32[256,1,1,512]{3,2,1,0:T(1,128)}), f32[256,1,1,512]{3,2,1,0:T(1,128)S(1)}, u32[]{:S(2)}, u32[]{:S(2)}) async-start(f32[256,1,1,512]{3,2,1,0:T(1,128)} %copy.16), calls=%async_computation.1 | async-start | bytes 1048576 | tf_op jit(solution)/shard_map/all_to_all | solution.py:49
  86.4 3.7 %all-gather.9 = s32[2,1,128]{2,1,0:T(1,128)S(1)} all-gather(s32[1,1,128]{2,1,0:T(1,128)S(1)} %bitcast.51), channel_id=9, replica_groups=mesh['chip_0'=4,'chip_1'=2,'board'=8,'cuts'=4] {'chip_1'}, dimensions={0}, use_global_device_ids=true | all-gather | bytes 1536 | tf_op jit(solution)/shard_map/all_gather | solution.py:26
  90.1 0.1 convert_element_type.26
  90.2 0.2 copy.17
  90.4 0.1 convert_element_type.28
  90.6 0.1 select_reduce_fusion
  90.7 0.7 dynamic_slice.4
  92.0 14.5 %all-to-all-done.1 = f32[256,1,1,512]{3,2,1,0:T(1,128)S(1)} async-done(((f32[256,1,1,512]{3,2,1,0:T(1,128)}), f32[256,1,1,512]{3,2,1,0:T(1,128)S(1)}, u32[]{:S(2)}, u32[]{:S(2)}) %all-to-all-start.1) | async-done | bytes 524320 | tf_op jit(solution)/shard_map/all_to_all | solution.py:49
  106.5 0.4 broadcast_divide_fusion
  106.9 0.9 div.30
  (10 shorter events, 0.1 us)
Async XLA Ops:
  0.7 1.2 %copy-start = (bf16[1,2048,256]{2,1,0:T(8,128)(2,1)S(1)}, bf16[1,2048,256]{2,1,0:T(8,128)(2,1)}, u32[]{:S(2)}) copy-start(bf16[1,2048,256]{2,1,0:T(8,128)(2,1)} %targ.1) | copy-start | bytes 3145732
  1.9 1.2 %copy-start.1 = (bf16[1,1024,512]{2,1,0:T(8,128)(2,1)S(1)}, bf16[1,1024,512]{2,1,0:T(8,128)(2,1)}, u32[]{:S(2)}) copy-start(bf16[1,1024,512]{2,1,0:T(8,128)(2,1)} %low.1) | copy-start | bytes 3145732
  3.1 1.0 copy-start.2
  4.1 0.7 copy-start.3
  4.8 32.6 %copy-start.6 = (u32[256]{0:T(256)S(1)}, u32[256]{0:T(256)}, u32[]{:S(2)}) copy-start(u32[256]{0:T(256)} %constant.21) | copy-start | bytes 3076
  4.8 42.2 %copy-start.5 = (u32[256]{0:T(256)S(1)}, u32[256]{0:T(256)}, u32[]{:S(2)}) copy-start(u32[256]{0:T(256)} %constant.31) | copy-start | bytes 3076
  4.8 42.8 %copy-start.4 = (u32[256]{0:T(256)S(1)}, u32[256]{0:T(256)}, u32[]{:S(2)}) copy-start(u32[256]{0:T(256)} %constant.26) | copy-start | bytes 3076
  21.1 57.7 %all-to-all-start = ((f32[256,1,1,512]{3,2,1,0:T(1,128)}), f32[256,1,1,512]{3,2,1,0:T(1,128)S(1)}, u32[]{:S(2)}, u32[]{:S(2)}) async-start(f32[256,1,1,512]{3,2,1,0:T(1,128)} %reshape_transpose_transpose_reshape_reshape_reshape.8), calls=%async_computation | async-start | bytes 1048576 | tf_op jit(solution)/shard_map/all_to_all | solution.py:49
  81.0 25.6 %all-to-all-start.1 = ((f32[256,1,1,512]{3,2,1,0:T(1,128)}), f32[256,1,1,512]{3,2,1,0:T(1,128)S(1)}, u32[]{:S(2)}, u32[]{:S(2)}) async-start(f32[256,1,1,512]{3,2,1,0:T(1,128)} %copy.16), calls=%async_computation.1 | async-start | bytes 1048576 | tf_op jit(solution)/shard_map/all_to_all | solution.py:49

commit v2 on v0

v2 whole, which is shorter than its diff:
```python
import functools
import math

import jax
import jax.numpy as jnp
from jax import lax
from jax.experimental import pallas as pl
from jax.experimental.pallas import tpu as pltpu
from jax.sharding import PartitionSpec as P

AXES = ("chip", "board", "cuts")
LR = 0.5
CLUSTERS = 8
LANES = 128
BLOCK = 512
PIECE = 256
MESH = pl.DeviceIdType.MESH
NN = (((1,), (0,)), ((), ()))
NT = (((1,), (1,)), ((), ()))
TN = (((0,), (0,)), ((), ()))


def product(a, b, dims):
    return lax.dot_general(a, b, dims, preferred_element_type=jnp.float32)


def split(value):
    high = value.astype(jnp.bfloat16)
    return high, (value - high.astype(jnp.float32)).astype(jnp.bfloat16)


def load_all(features, targets, lower, head, x_ref, t_ref, v_ref, w_ref, sems):
    block = min(BLOCK, x_ref.shape[0])
    blocks = x_ref.shape[0] // block
    pairs = [(lower.at[0], v_ref)]
    for k in range(blocks):
        rows = pl.ds(k * block, block)
        pairs.append((features.at[0, rows], x_ref.at[rows]))
    pairs += [(head.at[0], w_ref), (targets.at[0], t_ref)]
    copies = [pltpu.make_async_copy(src, dst, sems.at[k]) for k, (src, dst) in enumerate(pairs)]
    for copy in copies:
        copy.start()
    return copies


def count_draws(rows, m_ref):
    drawn = rows.shape[2]
    for step in range(rows.shape[1]):
        index = rows[0, pl.ds(step, 1), :]
        inner = lax.broadcasted_iota(jnp.int32, (LANES, drawn), 0) == index % LANES
        outer = lax.broadcasted_iota(jnp.int32, (m_ref.shape[2], drawn), 0) == index // LANES
        m_ref[step] = product(
            inner.astype(jnp.float32).astype(jnp.bfloat16),
            outer.astype(jnp.float32).astype(jnp.bfloat16),
            NT,
        )


def hidden_rows(copies, x_ref, v_ref, hh_ref, hl_ref):
    copies[0].wait()
    blocks = len(copies) - 3
    block = x_ref.shape[0] // blocks
    for k in range(blocks):
        copies[1 + k].wait()
        rows = pl.ds(k * block, block)
        hh_ref[rows], hl_ref[rows] = split(jnp.tanh(product(x_ref[rows], v_ref[...], NN)))


def local_step(step, weight, m_ref, t_ref, hh_ref, hl_ref, eh_ref, el_ref, drawn):
    wh, wl = split(weight)
    pool = hh_ref.shape[0]
    piece = min(PIECE, pool)
    per = piece // LANES
    for k in range(pool // piece):
        rows = pl.ds(k * piece, piece)
        high, low = hh_ref[rows], hl_ref[rows]
        err = product(high, wh, NN) + product(low, wh, NN) + product(high, wl, NN)
        err = err - t_ref[rows].astype(jnp.float32)
        err = jnp.concatenate(
            [
                err[q * LANES : (q + 1) * LANES] * m_ref[step, :, pl.ds(k * per + q, 1)]
                for q in range(per)
            ],
            0,
        )
        eh_ref[rows], el_ref[rows] = split(err)
    high, low = eh_ref[...], el_ref[...]
    grad = product(high, hh_ref[...], TN) + product(high, hl_ref[...], TN)
    grad = grad + product(low, hh_ref[...], TN)
    return grad.T * (-LR / drawn)


def kernel(
    sizes,
    features, targets, lower, head, rows, count, cluster,
    out,
    x_ref, t_ref, v_ref, w_ref, hh_ref, hl_ref, eh_ref, el_ref, m_ref,
    delta, mine, meta, part, parts, got1, sums, got2, totals, picked,
    load_sems, meta_send, meta_recv, part_send, part_recv,
    send1, recv1, send2, recv2, send3, recv3, send4, recv4,
):
    nc, nb, nx = sizes
    plane = nc * nx
    chunks = delta.shape[0]
    share = delta.shape[1] // plane
    c, b, x = (lax.axis_index(a) for a in AXES)
    me = c * nx + x

    def ahead(d):
        return (lax.rem(c + d // nx, nc), b, lax.rem(x + lax.rem(d, nx), nx))

    def behind(d):
        return (lax.rem(c + nc - d // nx, nc), b, lax.rem(x + nx - lax.rem(d, nx), nx))

    def along(e):
        return (c, lax.rem(b + e, nb), x)

    def remote(src, dst, send, recv, device):
        return pltpu.make_async_remote_copy(
            src_ref=src, dst_ref=dst, send_sem=send, recv_sem=recv, device_id=device, device_id_type=MESH
        )

    def loop(lo, hi, body):
        def run(k, carry):
            body(k)
            return carry

        lax.fori_loop(lo, hi, run, 0)

    copies = load_all(features, targets, lower, head, x_ref, t_ref, v_ref, w_ref, load_sems)
    barrier = pltpu.get_barrier_semaphore()
    loop(1, plane, lambda d: pl.semaphore_signal(barrier, inc=1, device_id=ahead(d), device_id_type=MESH))
    loop(1, nb, lambda e: pl.semaphore_signal(barrier, inc=1, device_id=along(e), device_id_type=MESH))
    count_draws(rows, m_ref)
    hidden_rows(copies, x_ref, v_ref, hh_ref, hl_ref)
    copies[-2].wait()
    copies[-1].wait()
    drawn = rows.shape[2]
    start = w_ref[...]
    first = local_step(0, start, m_ref, t_ref, hh_ref, hl_ref, eh_ref, el_ref, drawn)

    place = lax.broadcasted_iota(jnp.int32, mine.shape, 0) == cluster[0]
    mine[...] = jnp.where(place, count[0].astype(jnp.float32), 0.0)
    pl.semaphore_wait(barrier, plane - 1 + nb - 1)
    def meta_copy(d, device):
        return remote(mine, meta.at[d - 1], meta_send, meta_recv.at[d - 1], device)

    loop(1, plane, lambda d: meta_copy(d, ahead(d)).start())

    change = first + local_step(1, start + first, m_ref, t_ref, hh_ref, hl_ref, eh_ref, el_ref, drawn)
    for h in range(chunks):
        delta[h] = change[:, h * LANES : (h + 1) * LANES]

    def copy1(h, d):
        peer = ahead(d)
        at = pl.multiple_of((peer[0] * nx + peer[2]) * share, share)
        return remote(delta.at[h, pl.ds(at, share)], got1.at[h, d - 1], send1.at[h], recv1.at[h, d - 1], peer)

    for h in range(chunks):
        loop(1, plane, lambda d: copy1(h, d).start())

    def add_meta(d, total):
        meta_copy(d, ahead(d)).wait_recv()
        return total + meta[d - 1]

    part[...] = lax.fori_loop(1, plane, add_meta, mine[...])

    def part_copy(e):
        return remote(part, parts.at[e - 1], part_send, part_recv.at[e - 1], along(e))

    loop(1, nb, lambda e: part_copy(e).start())

    own = pl.multiple_of(me * share, share)

    def copy2(h, e):
        peer = along(e)
        return remote(sums.at[h, peer[1]], got2.at[h, e - 1], send2.at[h], recv2.at[h, e - 1], peer)

    for h in range(chunks):
        def add_share(d, acc):
            copy1(h, d).wait_recv()
            value = got1[h, d - 1]
            return tuple(a + value * meta[d - 1, pl.ds(k, 1), :] for k, a in enumerate(acc))

        value = delta[h, pl.ds(own, share)]
        acc = tuple(value * mine[pl.ds(k, 1), :] for k in range(CLUSTERS))
        acc = lax.fori_loop(1, plane, add_share, acc)
        for k in range(CLUSTERS):
            sums[h, k] = acc[k]
        loop(1, nb, lambda e: copy2(h, e).start())

    def copy3(h, e):
        return remote(totals.at[h, b], totals.at[h, b], send3.at[h], recv3.at[h, e - 1], along(e))

    for h in range(chunks):
        def add_sum(e, acc):
            copy2(h, e).wait_recv()
            return acc + got2[h, e - 1]

        totals[h, b] = lax.fori_loop(1, nb, add_sum, sums[h, b])
        loop(1, nb, lambda e: copy3(h, e).start())

    def add_part(e, acc):
        part_copy(e).wait_recv()
        return acc + parts[e - 1]

    counts = lax.fori_loop(1, nb, add_part, part[...])
    scale = 1.0 / (LR * counts)

    def copy4(h, d):
        target = out.at[pl.ds(own, share), pl.ds(h * LANES, LANES)]
        return remote(picked.at[h, d - 1], target, send4.at[h], recv4.at[h, d - 1], behind(d))

    for h in range(chunks):
        loop(1, nb, lambda e: copy3(h, e).wait_recv())
        means = [totals[h, k] * scale[k : k + 1, :] for k in range(CLUSTERS)]

        def choose(tile):
            value = jnp.zeros_like(means[0])
            for k in range(CLUSTERS):
                value = jnp.where(tile[k : k + 1, :] > 0.0, means[k], value)
            return value

        def give(d):
            picked[h, d - 1] = choose(meta[d - 1])
            copy4(h, d).start()

        loop(1, plane, give)
        out[pl.ds(own, share), pl.ds(h * LANES, LANES)] = choose(mine[...])

    for h in range(chunks):
        loop(1, plane, lambda d: copy4(h, d).wait_recv())

    loop(1, plane, lambda d: meta_copy(d, ahead(d)).wait_send())
    loop(1, nb, lambda e: part_copy(e).wait_send())
    for h in range(chunks):
        loop(1, plane, lambda d: copy1(h, d).wait_send())
        loop(1, nb, lambda e: copy2(h, e).wait_send())
        loop(1, nb, lambda e: copy3(h, e).wait_send())
        loop(1, plane, lambda d: copy4(h, d).wait_send())


def on_device(sizes, features, targets, lower_weight, head_weight, batch_rows, sample_counts, cluster_ids):
    nc, nb, nx = sizes
    plane = nc * nx
    _, pool, inside = features.shape
    _, hid, outs = head_weight.shape
    steps = batch_rows.shape[1]
    chunks = outs // LANES
    share = hid // plane
    blocks = pool // min(BLOCK, pool)
    hbm = pl.BlockSpec(memory_space=pltpu.HBM)
    vmem = pl.BlockSpec(memory_space=pltpu.VMEM)
    smem = pl.BlockSpec(memory_space=pltpu.SMEM)
    dma = pltpu.SemaphoreType.DMA
    f32, bf16 = jnp.float32, jnp.bfloat16
    result = pl.pallas_call(
        functools.partial(kernel, sizes),
        out_shape=jax.ShapeDtypeStruct((hid, outs), f32),
        in_specs=[hbm, hbm, hbm, hbm, vmem, smem, smem],
        out_specs=vmem,
        scratch_shapes=[
            pltpu.VMEM((pool, inside), bf16),
            pltpu.VMEM((pool, outs), bf16),
            pltpu.VMEM((inside, hid), bf16),
            pltpu.VMEM((hid, outs), f32),
            pltpu.VMEM((pool, hid), bf16),
            pltpu.VMEM((pool, hid), bf16),
            pltpu.VMEM((pool, outs), bf16),
            pltpu.VMEM((pool, outs), bf16),
            pltpu.VMEM((steps, LANES, pool // LANES), f32),
            pltpu.VMEM((chunks, hid, LANES), f32),
            pltpu.VMEM((CLUSTERS, LANES), f32),
            pltpu.VMEM((plane - 1, CLUSTERS, LANES), f32),
            pltpu.VMEM((CLUSTERS, LANES), f32),
            pltpu.VMEM((nb - 1, CLUSTERS, LANES), f32),
            pltpu.VMEM((chunks, plane - 1, share, LANES), f32),
            pltpu.VMEM((chunks, CLUSTERS, share, LANES), f32),
            pltpu.VMEM((chunks, nb - 1, share, LANES), f32),
            pltpu.VMEM((chunks, CLUSTERS, share, LANES), f32),
            pltpu.VMEM((chunks, plane - 1, share, LANES), f32),
            dma((blocks + 3,)),
            dma, dma((plane - 1,)), dma, dma((nb - 1,)),
            dma((chunks,)), dma((chunks, plane - 1)),
            dma((chunks,)), dma((chunks, nb - 1)),
            dma((chunks,)), dma((chunks, nb - 1)),
            dma((chunks,)), dma((chunks, plane - 1)),
        ],
        compiler_params=pltpu.CompilerParams(
            collective_id=0, has_side_effects=True, vmem_limit_bytes=64000 * 1024
        ),
    )(features, targets, lower_weight, head_weight, batch_rows, sample_counts, cluster_ids)
    return result[None]


def solution(mesh):
    sizes = tuple(mesh.shape[a] for a in AXES)
    whole = P(AXES)
    matrix = P(AXES, None, None)
    return jax.shard_map(
        functools.partial(on_device, sizes),
        mesh=mesh,
        in_specs=(matrix, matrix, matrix, matrix, matrix, whole, whole),
        out_specs=matrix,
        check_vma=False,
    )
```

time: 134 us -> 51.2 us (0.38)
  Pallas kernels: 0 us -> 47.9 us
  blocking collectives: 38.4 us -> 0 us
  local copies, waits for them, and re-layouts: 34.8 us -> 1.87 us
  starting transfers between devices: 21.1 us -> 0 us
  matrix products: 20.7 us -> 0 us
  waiting for transfers between devices: 14.5 us -> 0 us
  between operations: 3.45 us -> 1.3 us
    pallas_call x0 -> x1, Pallas kernels: none -> 47.9 us  [on_device(): pl.pallas_call(functools.partial(kernel, sizes), out_shape=jax.ShapeDtype...]
    unnamed x3 -> x0, blocking collectives: 26.9 us -> none
    gather x4 -> x0, local copies, waits for them, and re-layouts: 24 us -> none  [the longest x2 15.1 us: on_device(): picked = jnp.take(hidden, batch_rows[0, step], axis=0)]
    all_to_all x2 -> x0, starting transfers between devices: 21.1 us -> none  [exchange_both(): lax.all_to_all(blocks, axis, split_axis=0, concat_axis=0, tiled=True)]
    dot_general x7 -> x0, matrix products: 20.7 us -> none  [the longest x2 7.28 us: on_device(): grad = jnp.dot(picked.T, err, precision=lax.Precision.HIGHEST) / count_rows]
    all_to_all x2 -> x0, waiting for transfers between devices: 14.5 us -> none  [exchange_both(): lax.all_to_all(blocks, axis, split_axis=0, concat_axis=0, tiled=True)]
    all_gather x2 -> x0, blocking collectives: 11.5 us -> none  [gather_in_order(): blocks = lax.all_gather(blocks, axes[k], axis=0, tiled=True)]
    another operation x2 -> x0, local copies, waits for them, and re-layouts: 2.66 us -> none  [exchange_both(): blocks = blocks.reshape(-1, *inside)]
  transfers between devices with their start and end apart: 2 -> 0, of which waited for: 1 -> 0; matrix products, arithmetic and copies ran while one was open for 5% -> 0% of each run, Pallas kernels for 0% -> 0%
where the time goes in v2:
time: 51.2 us; the launch traced here: 51 us
  Pallas kernels  47.9 us (94%)
  local copies, waits for them, and re-layouts  1.87 us (4%)
  between operations  1.3 us (3%)
    pallas_call x1, Pallas kernels, on_device(): pl.pallas_call(functools.partial(kernel, sizes), out_shape=jax.ShapeDtype...  47.9 us
    unnamed x1, local copies, waits for them, and re-layouts  1.87 us

profile of v2, /device:TPU:1, one launch (start us, length us, event | category | flops | bytes accessed | tf_op | source)
XLA Modules:
  0.0 51.0 jit_solution(10668561459373686768)
XLA Ops:
  1.3 47.9 %shard_map.73 = f32[512,256]{1,0:T(8,128)} custom-call(bf16[1,2048,1024]{2,1,0:T(8,128)(2,1)} %features.1, bf16[1,2048,256]{2,1,0:T(8,128)(2,1)} %targets.1, bf16[1,1024,512]{2,1,0:T(8,128)(2,1)} %lower.1, f32[1,512,256]{2,1,0:T(8,128)} %head.1, s32[1,2,1024]{2,1,0:T(2,128)} %rows.1, s32[1]{0:T(128)S(6)} %copy.9.count, s32[1]{0:T(128)S(6)} %copy.10.cluster), custom_call_target="tpu_custom_call" | custom-call | tf_op jit(solution)/shard_map/pallas_call | solution.py:257
  49.2 1.9 %copy.11 = f32[1,512,256]{2,1,0:T(8,128)} copy(f32[1,512,256]{2,1,0:T(8,128)} %bitcast.1) | data formatting | bytes 1048576

commit v3 on v2

v3 whole, which is shorter than its diff:
```python
import functools
import math

import jax
import jax.numpy as jnp
from jax import lax
from jax.experimental import pallas as pl
from jax.experimental.pallas import tpu as pltpu
from jax.sharding import PartitionSpec as P

AXES = ("chip", "board", "cuts")
LR = 0.5
CLUSTERS = 8
LANES = 128
BLOCK = 512
PIECE = 256
SUBLANES = 8
SPLIT_COLUMNS = False
GRANT = 64000 * 1024
MESH = pl.DeviceIdType.MESH
NN = (((1,), (0,)), ((), ()))
NT = (((1,), (1,)), ((), ()))
TN = (((0,), (0,)), ((), ()))


def product(a, b, dims):
    return lax.dot_general(a, b, dims, preferred_element_type=jnp.float32)


def split(value):
    high = value.astype(jnp.bfloat16)
    return high, (value - high.astype(jnp.float32)).astype(jnp.bfloat16)


def load_all(pairs, sems):
    copies = [pltpu.make_async_copy(src, dst, sems.at[k]) for k, (src, dst) in enumerate(pairs)]
    for copy in copies:
        copy.start()
    return copies


def count_draws(rows, m_ref):
    steps, drawn = rows.shape
    for step in range(steps):
        index = rows[pl.ds(step, 1), :]
        inner = lax.broadcasted_iota(jnp.int32, (LANES, drawn), 0) == index % LANES
        outer = lax.broadcasted_iota(jnp.int32, (m_ref.shape[2], drawn), 0) == index // LANES
        m_ref[step] = product(
            inner.astype(jnp.float32).astype(jnp.bfloat16),
            outer.astype(jnp.float32).astype(jnp.bfloat16),
            NT,
        )


def errors(step, weight, columns, m_ref, t_ref, hh_ref, hl_ref, e_ref):
    wh, wl = split(weight)
    wide = weight.shape[1]
    pool = hh_ref.shape[0]
    piece = min(PIECE, pool)
    per = piece // LANES
    for k in range(pool // piece):
        rows = pl.ds(k * piece, piece)
        high, low = hh_ref[rows], hl_ref[rows]
        if wide == LANES:
            both = product(high, jnp.concatenate([wh, wl], 1), NN)
            err = both[:, :wide] + both[:, wide:] + product(low, wh, NN)
        else:
            err = product(high, wh, NN) + product(low, wh, NN) + product(high, wl, NN)
        err = err - t_ref[rows, columns].astype(jnp.float32)
        err = jnp.concatenate(
            [
                err[q * LANES : (q + 1) * LANES] * m_ref[step, :, pl.ds(k * per + q, 1)]
                for q in range(per)
            ],
            0,
        )
        e_ref[rows, :wide], e_ref[rows, wide : 2 * wide] = split(err)


def gradient(wide, rows, hh_ref, hl_ref, e_ref):
    high = hh_ref[:, rows]
    if wide == LANES:
        both = product(e_ref[:, : 2 * wide], high, TN)
        grad = both[:wide] + both[wide:] + product(e_ref[:, :wide], hl_ref[:, rows], TN)
    else:
        grad = product(e_ref[:, :wide], high, TN) + product(e_ref[:, :wide], hl_ref[:, rows], TN)
        grad = grad + product(e_ref[:, wide : 2 * wide], high, TN)
    return grad.T


def kernel(
    sizes,
    features, targets, lower, head, rows, count, cluster,
    out,
    x_ref, t_ref, v_ref, w_ref, hh_ref, hl_ref, e_ref, m_ref, rows_ref, count_ref, cluster_ref,
    delta, mine, meta, part, parts, got1, sums, got2, totals, picked,
    load_sems, meta_send, meta_recv, part_send, part_recv,
    send1, recv1, send2, recv2, send3, recv3, send4, recv4,
):
    nc, nb, nx = sizes
    plane = nc * nx
    chunks = delta.shape[0]
    share = SUBLANES
    hid, outs = w_ref.shape
    half = share * plane
    c, b, x = (lax.axis_index(a) for a in AXES)
    own = pl.multiple_of((c * nx + x) * share, share)

    def ahead(d):
        return (lax.rem(c + d // nx, nc), b, lax.rem(x + lax.rem(d, nx), nx))

    def behind(d):
        return (lax.rem(c + nc - d // nx, nc), b, lax.rem(x + nx - lax.rem(d, nx), nx))

    def along(e):
        return (c, lax.rem(b + e, nb), x)

    def steps_of(d, n):
        return min(d, n - d)

    order = sorted(
        range(1, plane),
        key=lambda d: -steps_of(d // nx // 2, max(nc // 2, 1)) - steps_of(d % nx, nx),
    )

    def remote(src, dst, send, recv, device):
        return pltpu.make_async_remote_copy(
            src_ref=src, dst_ref=dst, send_sem=send, recv_sem=recv, device_id=device, device_id_type=MESH
        )

    def loop(lo, hi, body):
        def run(k, carry):
            body(k)
            return carry

        lax.fori_loop(lo, hi, run, 0)

    def done(ref, sem):
        pltpu.make_async_copy(ref, ref, sem).wait()

    block = min(BLOCK, x_ref.shape[0])
    blocks = x_ref.shape[0] // block
    pairs = [(rows.at[0], rows_ref), (lower.at[0], v_ref)]
    for k in range(blocks):
        pairs.append((features.at[0, pl.ds(k * block, block)], x_ref.at[pl.ds(k * block, block)]))
    pairs += [(head.at[0], w_ref), (targets.at[0], t_ref), (count, count_ref), (cluster, cluster_ref)]
    copies = load_all(pairs, load_sems)
    barrier = pltpu.get_barrier_semaphore()
    loop(1, plane, lambda d: pl.semaphore_signal(barrier, inc=1, device_id=ahead(d), device_id_type=MESH))
    loop(1, nb, lambda e: pl.semaphore_signal(barrier, inc=1, device_id=along(e), device_id_type=MESH))
    copies[0].wait()
    count_draws(rows_ref, m_ref)
    copies[1].wait()
    for k in range(blocks):
        copies[2 + k].wait()
        here = pl.ds(k * block, block)
        hh_ref[here], hl_ref[here] = split(jnp.tanh(product(x_ref[here], v_ref[...], NN)))
    for copy in copies[2 + blocks :]:
        copy.wait()

    place = lax.broadcasted_iota(jnp.int32, mine.shape, 0) == cluster_ref[0]
    mine[...] = jnp.where(place, count_ref[0].astype(jnp.float32), 0.0)

    def meta_copy(d):
        return remote(mine, meta.at[d - 1], meta_send, meta_recv, ahead(d))

    def copy1(h, d):
        peer = ahead(d)
        at = pl.multiple_of((peer[0] * nx + peer[2]) * share, share)
        return remote(delta.at[h, pl.ds(at, share)], got1.at[h, d - 1], send1.at[h], recv1.at[h], peer)

    drawn = rows_ref.shape[1]
    rate = -LR / drawn
    wide = LANES if SPLIT_COLUMNS else outs
    tiles = wide // LANES
    h = 0
    places = []
    for col in range(0, outs, wide):
        columns = slice(col, col + wide)
        start = w_ref[:, columns]
        errors(0, start, columns, m_ref, t_ref, hh_ref, hl_ref, e_ref)
        first = gradient(wide, slice(None), hh_ref, hl_ref, e_ref) * rate
        if col == 0:
            pl.semaphore_wait(barrier, plane - 1 + nb - 1)
            loop(1, plane, lambda d: meta_copy(d).start())
        errors(1, start + first, columns, m_ref, t_ref, hh_ref, hl_ref, e_ref)
        for row in range(0, hid, half):
            change = first[row : row + half] + gradient(wide, slice(row, row + half), hh_ref, hl_ref, e_ref) * rate
            for t in range(tiles):
                delta[h] = change[:, t * LANES : (t + 1) * LANES]
                places.append((row, col + t * LANES))
                for d in order:
                    copy1(h, d).start()
                h += 1

    done(meta, meta_recv)
    part[...] = mine[...] + jnp.sum(meta[...], axis=0)

    def part_copy(e):
        return remote(part, parts.at[e - 1], part_send, part_recv, along(e))

    loop(1, nb, lambda e: part_copy(e).start())

    def copy2(h, e):
        peer = along(e)
        return remote(sums.at[h, peer[1]], got2.at[h, e - 1], send2.at[h], recv2.at[h], peer)

    def copy3(h, e):
        return remote(totals.at[h, b], totals.at[h, b], send3.at[h], recv3.at[h], along(e))

    def target(h):
        row, col = places[h]
        return out.at[pl.ds(row + own, share), pl.ds(col, LANES)]

    def copy4(h, d):
        return remote(picked.at[h, d - 1], target(h), send4.at[h], recv4.at[h], behind(d))

    def stage1(h):
        done(got1.at[h], recv1.at[h])
        value = delta[h, pl.ds(own, share)]
        got = got1[h]
        for k in range(CLUSTERS):
            sums[h, k] = value * mine[pl.ds(k, 1), :] + jnp.sum(got * meta[:, k : k + 1, :], axis=0)
        loop(1, nb, lambda e: copy2(h, e).start())

    def stage2(h):
        done(got2.at[h], recv2.at[h])
        totals[h, b] = sums[h, b] + jnp.sum(got2[h], axis=0)
        loop(1, nb, lambda e: copy3(h, e).start())

    def stage3(h, scale):
        done(got2.at[h], recv3.at[h])
        value = jnp.zeros(picked.shape[1:], jnp.float32)
        kept = jnp.zeros((share, LANES), jnp.float32)
        for k in range(CLUSTERS):
            mean = totals[h, k] * scale[k : k + 1, :]
            value = jnp.where(meta[:, k : k + 1, :] > 0.0, mean[None], value)
            kept = jnp.where(mine[pl.ds(k, 1), :] > 0.0, mean, kept)
        picked[h] = value
        for d in order:
            copy4(h, d).start()
        row, col = places[h]
        out[pl.ds(row + own, share), pl.ds(col, LANES)] = kept

    for h in range(chunks):
        stage1(h)
    for h in range(chunks):
        stage2(h)
    done(parts, part_recv)
    scale = 1.0 / (LR * (part[...] + jnp.sum(parts[...], axis=0)))
    for h in range(chunks):
        stage3(h, scale)
    for h in range(chunks):
        done(got1.at[h], recv4.at[h])

    done(meta, meta_send)
    done(parts, part_send)
    for h in range(chunks):
        done(got1.at[h], send1.at[h])
        done(got2.at[h], send2.at[h])
        done(got2.at[h], send3.at[h])
        done(got1.at[h], send4.at[h])


def on_device(sizes, features, targets, lower_weight, head_weight, batch_rows, sample_counts, cluster_ids):
    nc, nb, nx = sizes
    plane = nc * nx
    _, pool, inside = features.shape
    _, hid, outs = head_weight.shape
    _, steps, drawn = batch_rows.shape
    share = SUBLANES
    chunks = hid // (plane * share) * (outs // LANES)
    blocks = pool // min(BLOCK, pool)
    hbm = pl.BlockSpec(memory_space=pltpu.HBM)
    vmem = pl.BlockSpec(memory_space=pltpu.VMEM)
    dma = pltpu.SemaphoreType.DMA
    f32, bf16 = jnp.float32, jnp.bfloat16
    result = pl.pallas_call(
        functools.partial(kernel, sizes),
        out_shape=jax.ShapeDtypeStruct((hid, outs), f32),
        in_specs=[hbm] * 7,
        out_specs=vmem,
        scratch_shapes=[
            pltpu.VMEM((pool, inside), bf16),
            pltpu.VMEM((pool, outs), bf16),
            pltpu.VMEM((inside, hid), bf16),
            pltpu.VMEM((hid, outs), f32),
            pltpu.VMEM((pool, hid), bf16),
            pltpu.VMEM((pool, hid), bf16),
            pltpu.VMEM((pool, 2 * outs), bf16),
            pltpu.VMEM((steps, LANES, pool // LANES), f32),
            pltpu.VMEM((steps, drawn), jnp.int32),
            pltpu.SMEM((1,), jnp.int32),
            pltpu.SMEM((1,), jnp.int32),
            pltpu.VMEM((chunks, plane * share, LANES), f32),
            pltpu.VMEM((CLUSTERS, LANES), f32),
            pltpu.VMEM((plane - 1, CLUSTERS, LANES), f32),
            pltpu.VMEM((CLUSTERS, LANES), f32),
            pltpu.VMEM((nb - 1, CLUSTERS, LANES), f32),
            pltpu.VMEM((chunks, plane - 1, share, LANES), f32),
            pltpu.VMEM((chunks, CLUSTERS, share, LANES), f32),
            pltpu.VMEM((chunks, nb - 1, share, LANES), f32),
            pltpu.VMEM((chunks, CLUSTERS, share, LANES), f32),
            pltpu.VMEM((chunks, plane - 1, share, LANES), f32),
            dma((blocks + 6,)),
            dma, dma, dma, dma,
            *[dma((chunks,)) for _ in range(8)],
        ],
        compiler_params=pltpu.CompilerParams(
            collective_id=0, has_side_effects=True, vmem_limit_bytes=GRANT
        ),
    )(features, targets, lower_weight, head_weight, batch_rows, sample_counts, cluster_ids)
    return result[None]


def solution(mesh):
    sizes = tuple(mesh.shape[a] for a in AXES)
    whole = P(AXES)
    matrix = P(AXES, None, None)
    return jax.shard_map(
        functools.partial(on_device, sizes),
        mesh=mesh,
        in_specs=(matrix, matrix, matrix, matrix, matrix, whole, whole),
        out_specs=matrix,
        check_vma=False,
    )
```

time: 51.2 us -> 46.6 us (0.910)
  Pallas kernels: 47.9 us -> 43.3 us
    pallas_call x1, Pallas kernels: 47.9 us -> 43.3 us  [on_device(): pl.pallas_call(functools.partial(kernel, sizes), out_shape=jax.ShapeDtype...]
where the time goes in v3:
time: 46.6 us; the launch traced here: 46.5 us
  Pallas kernels  43.3 us (93%)
  local copies, waits for them, and re-layouts  1.87 us (4%)
  between operations  1.3 us (3%)
    pallas_call x1, Pallas kernels, on_device(): pl.pallas_call(functools.partial(kernel, sizes), out_shape=jax.ShapeDtype...  43.3 us
    unnamed x1, local copies, waits for them, and re-layouts  1.87 us

profile of v3, /device:TPU:1, one launch (start us, length us, event | category | flops | bytes accessed | tf_op | source)
XLA Modules:
  0.0 46.5 jit_solution(11500601653462048759)
XLA Ops:
  1.3 43.3 %shard_map.73 = f32[512,256]{1,0:T(8,128)} custom-call(bf16[1,2048,1024]{2,1,0:T(8,128)(2,1)} %features.1, bf16[1,2048,256]{2,1,0:T(8,128)(2,1)} %targets.1, bf16[1,1024,512]{2,1,0:T(8,128)(2,1)} %lower.1, f32[1,512,256]{2,1,0:T(8,128)} %head.1, s32[1,2,1024]{2,1,0:T(2,128)} %rows.1, s32[1]{0:T(128)S(6)} %copy.9.count, s32[1]{0:T(128)S(6)} %copy.10.cluster), custom_call_target="tpu_custom_call" | custom-call | tf_op jit(solution)/shard_map/pallas_call | solution.py:278
  44.6 1.9 %copy.11 = f32[1,512,256]{2,1,0:T(8,128)} copy(f32[1,512,256]{2,1,0:T(8,128)} %bitcast.1) | data formatting | bytes 1048576

commit v4 on v3

--- a/solution.py
+++ b/solution.py
@@ -16,7 +16,7 @@
 PIECE = 256
 SUBLANES = 8
 SPLIT_COLUMNS = False
-GRANT = 64000 * 1024
+GRANT = 48000 * 1024
 MESH = pl.DeviceIdType.MESH
 NN = (((1,), (0,)), ((), ()))
 NT = (((1,), (1,)), ((), ()))
@@ -90,10 +90,10 @@
 
 def kernel(
     sizes,
-    features, targets, lower, head, rows, count, cluster,
+    features, targets, lower, head, rows, mine,
     out,
-    x_ref, t_ref, v_ref, w_ref, hh_ref, hl_ref, e_ref, m_ref, rows_ref, count_ref, cluster_ref,
-    delta, mine, meta, part, parts, got1, sums, got2, totals, picked,
+    x_ref, t_ref, v_ref, w_ref, hh_ref, hl_ref, e_ref, m_ref, rows_ref,
+    delta, meta, part, parts, got1, sums, got2, totals, picked,
     load_sems, meta_send, meta_recv, part_send, part_recv,
     send1, recv1, send2, recv2, send3, recv3, send4, recv4,
 ):
@@ -143,7 +143,7 @@
     pairs = [(rows.at[0], rows_ref), (lower.at[0], v_ref)]
     for k in range(blocks):
         pairs.append((features.at[0, pl.ds(k * block, block)], x_ref.at[pl.ds(k * block, block)]))
-    pairs += [(head.at[0], w_ref), (targets.at[0], t_ref), (count, count_ref), (cluster, cluster_ref)]
+    pairs += [(head.at[0], w_ref), (targets.at[0], t_ref)]
     copies = load_all(pairs, load_sems)
     barrier = pltpu.get_barrier_semaphore()
     loop(1, plane, lambda d: pl.semaphore_signal(barrier, inc=1, device_id=ahead(d), device_id_type=MESH))
@@ -153,13 +153,11 @@
     copies[1].wait()
     for k in range(blocks):
         copies[2 + k].wait()
+        if k == blocks - 1:
+            for copy in copies[2 + blocks :]:
+                copy.wait()
         here = pl.ds(k * block, block)
         hh_ref[here], hl_ref[here] = split(jnp.tanh(product(x_ref[here], v_ref[...], NN)))
-    for copy in copies[2 + blocks :]:
-        copy.wait()
-
-    place = lax.broadcasted_iota(jnp.int32, mine.shape, 0) == cluster_ref[0]
-    mine[...] = jnp.where(place, count_ref[0].astype(jnp.float32), 0.0)
 
     def meta_copy(d):
         return remote(mine, meta.at[d - 1], meta_send, meta_recv, ahead(d))
@@ -275,10 +273,16 @@
     vmem = pl.BlockSpec(memory_space=pltpu.VMEM)
     dma = pltpu.SemaphoreType.DMA
     f32, bf16 = jnp.float32, jnp.bfloat16
+    place = lax.broadcasted_iota(jnp.int32, (CLUSTERS, LANES), 0) == cluster_ids[0]
+    mine = jnp.where(place, sample_counts[0].astype(f32), 0.0)
+    held = [
+        pltpu.with_memory_space_constraint(v, pltpu.HBM)
+        for v in (features, targets, lower_weight, head_weight, batch_rows)
+    ]
     result = pl.pallas_call(
         functools.partial(kernel, sizes),
         out_shape=jax.ShapeDtypeStruct((hid, outs), f32),
-        in_specs=[hbm] * 7,
+        in_specs=[hbm] * 5 + [vmem],
         out_specs=vmem,
         scratch_shapes=[
             pltpu.VMEM((pool, inside), bf16),
@@ -290,10 +294,7 @@
             pltpu.VMEM((pool, 2 * outs), bf16),
             pltpu.VMEM((steps, LANES, pool // LANES), f32),
             pltpu.VMEM((steps, drawn), jnp.int32),
-            pltpu.SMEM((1,), jnp.int32),
-            pltpu.SMEM((1,), jnp.int32),
             pltpu.VMEM((chunks, plane * share, LANES), f32),
-            pltpu.VMEM((CLUSTERS, LANES), f32),
             pltpu.VMEM((plane - 1, CLUSTERS, LANES), f32),
             pltpu.VMEM((CLUSTERS, LANES), f32),
             pltpu.VMEM((nb - 1, CLUSTERS, LANES), f32),
@@ -302,14 +303,14 @@
             pltpu.VMEM((chunks, nb - 1, share, LANES), f32),
             pltpu.VMEM((chunks, CLUSTERS, share, LANES), f32),
             pltpu.VMEM((chunks, plane - 1, share, LANES), f32),
-            dma((blocks + 6,)),
+            dma((blocks + 4,)),
             dma, dma, dma, dma,
             *[dma((chunks,)) for _ in range(8)],
         ],
         compiler_params=pltpu.CompilerParams(
             collective_id=0, has_side_effects=True, vmem_limit_bytes=GRANT
         ),
-    )(features, targets, lower_weight, head_weight, batch_rows, sample_counts, cluster_ids)
+    )(*held, mine)
     return result[None]
 
 

time: 46.6 us -> 44.5 us (0.955)
  Pallas kernels: 43.3 us -> 42.3 us
  local copies, waits for them, and re-layouts: 1.87 us -> 0.87 us
    unnamed x1, local copies, waits for them, and re-layouts: 1.87 us -> 0.8 us
    pallas_call x1, Pallas kernels: 43.3 us -> 42.3 us  [on_device(): pl.pallas_call(functools.partial(kernel, sizes), out_shape=jax.ShapeDtype...]
where the time goes in v4:
time: 44.5 us
  Pallas kernels  42.3 us (95%)
  between operations  1.31 us (3%)
  local copies, waits for them, and re-layouts  0.87 us (2%)
    pallas_call x1, Pallas kernels, on_device(): pl.pallas_call(functools.partial(kernel, sizes), out_shape=jax.ShapeDtype...  42.3 us

profile of v4, /device:TPU:1, one launch (start us, length us, event | category | flops | bytes accessed | tf_op | source)
XLA Modules:
  0.0 44.5 jit_solution(3041971783591526925)
XLA Ops:
  1.3 0.1 iota.7.mine
  1.4 42.3 %shard_map.73 = f32[512,256]{1,0:T(8,128)S(1)} custom-call(bf16[1,2048,1024]{2,1,0:T(8,128)(2,1)} %features.1, bf16[1,2048,256]{2,1,0:T(8,128)(2,1)} %targets.1, bf16[1,1024,512]{2,1,0:T(8,128)(2,1)} %lower.1, f32[1,512,256]{2,1,0:T(8,128)} %head.1, s32[1,2,1024]{2,1,0:T(2,128)} %rows.1, f32[8,128]{1,0:T(8,128)S(1)} %iota.7.mine), custom_call_target="tpu_custom_call" | custom-call | tf_op jit(solution)/shard_map/pallas_call | solution.py:282
  43.7 0.8 %copy.11 = f32[1,512,256]{2,1,0:T(8,128)} copy(f32[1,512,256]{2,1,0:T(8,128)S(1)} %bitcast.4) | data formatting | bytes 1048576
  (1 shorter events, 0.0 us)

commit v5 on v4

--- a/solution.py
+++ b/solution.py
@@ -13,9 +13,9 @@
 CLUSTERS = 8
 LANES = 128
 BLOCK = 512
-PIECE = 256
+PIECE = 512
 SUBLANES = 8
-SPLIT_COLUMNS = False
+WIDE = 128
 GRANT = 48000 * 1024
 MESH = pl.DeviceIdType.MESH
 NN = (((1,), (0,)), ((), ()))
@@ -44,48 +44,46 @@
     for step in range(steps):
         index = rows[pl.ds(step, 1), :]
         inner = lax.broadcasted_iota(jnp.int32, (LANES, drawn), 0) == index % LANES
-        outer = lax.broadcasted_iota(jnp.int32, (m_ref.shape[2], drawn), 0) == index // LANES
+        outer = lax.broadcasted_iota(jnp.int32, (m_ref.shape[1], drawn), 0) == index // LANES
         m_ref[step] = product(
+            outer.astype(jnp.float32).astype(jnp.bfloat16),
             inner.astype(jnp.float32).astype(jnp.bfloat16),
-            outer.astype(jnp.float32).astype(jnp.bfloat16),
             NT,
         )
 
 
 def errors(step, weight, columns, m_ref, t_ref, hh_ref, hl_ref, e_ref):
     wh, wl = split(weight)
-    wide = weight.shape[1]
+    outs = weight.shape[0]
     pool = hh_ref.shape[0]
     piece = min(PIECE, pool)
     per = piece // LANES
     for k in range(pool // piece):
         rows = pl.ds(k * piece, piece)
         high, low = hh_ref[rows], hl_ref[rows]
-        if wide == LANES:
-            both = product(high, jnp.concatenate([wh, wl], 1), NN)
-            err = both[:, :wide] + both[:, wide:] + product(low, wh, NN)
+        if outs == LANES:
+            err = product(high, jnp.concatenate([wh, wl], 0), NT)
+            err = err[:, :outs] + err[:, outs:] + product(low, wh, NT)
         else:
-            err = product(high, wh, NN) + product(low, wh, NN) + product(high, wl, NN)
-        err = err - t_ref[rows, columns].astype(jnp.float32)
+            err = product(high, wh, NT) + product(low, wh, NT) + product(high, wl, NT)
+        err = (err - t_ref[rows, columns].astype(jnp.float32)).T
         err = jnp.concatenate(
             [
-                err[q * LANES : (q + 1) * LANES] * m_ref[step, :, pl.ds(k * per + q, 1)]
+                err[:, q * LANES : (q + 1) * LANES] * m_ref[step, pl.ds(k * per + q, 1), :]
                 for q in range(per)
             ],
-            0,
+            1,
         )
-        e_ref[rows, :wide], e_ref[rows, wide : 2 * wide] = split(err)
-
-
-def gradient(wide, rows, hh_ref, hl_ref, e_ref):
+        e_ref[:outs, rows], e_ref[outs : 2 * outs, rows] = split(err)
+
+
+def gradient(outs, rows, hh_ref, hl_ref, e_ref):
     high = hh_ref[:, rows]
-    if wide == LANES:
-        both = product(e_ref[:, : 2 * wide], high, TN)
-        grad = both[:wide] + both[wide:] + product(e_ref[:, :wide], hl_ref[:, rows], TN)
-    else:
-        grad = product(e_ref[:, :wide], high, TN) + product(e_ref[:, :wide], hl_ref[:, rows], TN)
-        grad = grad + product(e_ref[:, wide : 2 * wide], high, TN)
-    return grad.T
+    if outs == LANES:
+        grad = product(e_ref[: 2 * outs], high, NN)
+        return grad[:outs] + grad[outs:] + product(e_ref[:outs], hl_ref[:, rows], NN)
+    grad = product(e_ref[:outs], high, NN) + product(e_ref[:outs], hl_ref[:, rows], NN)
+    return grad + product(e_ref[outs : 2 * outs], high, NN)
 
 
 def kernel(
@@ -123,6 +121,8 @@
         key=lambda d: -steps_of(d // nx // 2, max(nc // 2, 1)) - steps_of(d % nx, nx),
     )
 
+    z_order = sorted(range(1, nb), key=lambda e: -steps_of(e, nb))
+
     def remote(src, dst, send, recv, device):
         return pltpu.make_async_remote_copy(
             src_ref=src, dst_ref=dst, send_sem=send, recv_sem=recv, device_id=device, device_id_type=MESH
@@ -137,6 +137,9 @@
 
     def done(ref, sem):
         pltpu.make_async_copy(ref, ref, sem).wait()
+
+    def spread(value):
+        return jnp.concatenate([value] * (WIDE // LANES), axis=-1)
 
     block = min(BLOCK, x_ref.shape[0])
     blocks = x_ref.shape[0] // block
@@ -169,27 +172,23 @@
 
     drawn = rows_ref.shape[1]
     rate = -LR / drawn
-    wide = LANES if SPLIT_COLUMNS else outs
-    tiles = wide // LANES
     h = 0
     places = []
-    for col in range(0, outs, wide):
-        columns = slice(col, col + wide)
-        start = w_ref[:, columns]
-        errors(0, start, columns, m_ref, t_ref, hh_ref, hl_ref, e_ref)
-        first = gradient(wide, slice(None), hh_ref, hl_ref, e_ref) * rate
-        if col == 0:
-            pl.semaphore_wait(barrier, plane - 1 + nb - 1)
-            loop(1, plane, lambda d: meta_copy(d).start())
-        errors(1, start + first, columns, m_ref, t_ref, hh_ref, hl_ref, e_ref)
+    start = w_ref[...].T
+    errors(0, start, slice(0, outs), m_ref, t_ref, hh_ref, hl_ref, e_ref)
+    first = gradient(outs, slice(None), hh_ref, hl_ref, e_ref) * rate
+    pl.semaphore_wait(barrier, plane - 1 + nb - 1)
+    loop(1, plane, lambda d: meta_copy(d).start())
+    for col in range(0, outs, WIDE):
+        columns = slice(col, col + WIDE)
+        errors(1, (start + first)[columns], columns, m_ref, t_ref, hh_ref, hl_ref, e_ref)
         for row in range(0, hid, half):
-            change = first[row : row + half] + gradient(wide, slice(row, row + half), hh_ref, hl_ref, e_ref) * rate
-            for t in range(tiles):
-                delta[h] = change[:, t * LANES : (t + 1) * LANES]
-                places.append((row, col + t * LANES))
-                for d in order:
-                    copy1(h, d).start()
-                h += 1
+            change = gradient(WIDE, slice(row, row + half), hh_ref, hl_ref, e_ref) * rate
+            delta[h] = (first[columns, row : row + half] + change).T
+            places.append((row, col))
+            for d in order:
+                copy1(h, d).start()
+            h += 1
 
     done(meta, meta_recv)
     part[...] = mine[...] + jnp.sum(meta[...], axis=0)
@@ -208,7 +207,7 @@
 
     def target(h):
         row, col = places[h]
-        return out.at[pl.ds(row + own, share), pl.ds(col, LANES)]
+        return out.at[pl.ds(row + own, share), pl.ds(col, WIDE)]
 
     def copy4(h, d):
         return remote(picked.at[h, d - 1], target(h), send4.at[h], recv4.at[h], behind(d))
@@ -218,27 +217,29 @@
         value = delta[h, pl.ds(own, share)]
         got = got1[h]
         for k in range(CLUSTERS):
-            sums[h, k] = value * mine[pl.ds(k, 1), :] + jnp.sum(got * meta[:, k : k + 1, :], axis=0)
-        loop(1, nb, lambda e: copy2(h, e).start())
+            sums[h, k] = value * spread(mine[pl.ds(k, 1), :]) + jnp.sum(got * spread(meta[:, k : k + 1, :]), axis=0)
+        for e in z_order:
+            copy2(h, e).start()
 
     def stage2(h):
         done(got2.at[h], recv2.at[h])
         totals[h, b] = sums[h, b] + jnp.sum(got2[h], axis=0)
-        loop(1, nb, lambda e: copy3(h, e).start())
+        for e in z_order:
+            copy3(h, e).start()
 
     def stage3(h, scale):
         done(got2.at[h], recv3.at[h])
         value = jnp.zeros(picked.shape[1:], jnp.float32)
-        kept = jnp.zeros((share, LANES), jnp.float32)
+        kept = jnp.zeros((share, WIDE), jnp.float32)
         for k in range(CLUSTERS):
-            mean = totals[h, k] * scale[k : k + 1, :]
-            value = jnp.where(meta[:, k : k + 1, :] > 0.0, mean[None], value)
-            kept = jnp.where(mine[pl.ds(k, 1), :] > 0.0, mean, kept)
+            mean = totals[h, k] * spread(scale[k : k + 1, :])
+            value = jnp.where(spread(meta[:, k : k + 1, :]) > 0.0, mean[None], value)
+            kept = jnp.where(spread(mine[pl.ds(k, 1), :]) > 0.0, mean, kept)
         picked[h] = value
         for d in order:
             copy4(h, d).start()
         row, col = places[h]
-        out[pl.ds(row + own, share), pl.ds(col, LANES)] = kept
+        out[pl.ds(row + own, share), pl.ds(col, WIDE)] = kept
 
     for h in range(chunks):
         stage1(h)
@@ -267,7 +268,7 @@
     _, hid, outs = head_weight.shape
     _, steps, drawn = batch_rows.shape
     share = SUBLANES
-    chunks = hid // (plane * share) * (outs // LANES)
+    chunks = hid // (plane * share) * (outs // WIDE)
     blocks = pool // min(BLOCK, pool)
     hbm = pl.BlockSpec(memory_space=pltpu.HBM)
     vmem = pl.BlockSpec(memory_space=pltpu.VMEM)
@@ -291,18 +292,18 @@
             pltpu.VMEM((hid, outs), f32),
             pltpu.VMEM((pool, hid), bf16),
             pltpu.VMEM((pool, hid), bf16),
-            pltpu.VMEM((pool, 2 * outs), bf16),
-            pltpu.VMEM((steps, LANES, pool // LANES), f32),
+            pltpu.VMEM((2 * outs, pool), bf16),
+            pltpu.VMEM((steps, pool // LANES, LANES), f32),
             pltpu.VMEM((steps, drawn), jnp.int32),
-            pltpu.VMEM((chunks, plane * share, LANES), f32),
+            pltpu.VMEM((chunks, plane * share, WIDE), f32),
             pltpu.VMEM((plane - 1, CLUSTERS, LANES), f32),
             pltpu.VMEM((CLUSTERS, LANES), f32),
             pltpu.VMEM((nb - 1, CLUSTERS, LANES), f32),
-            pltpu.VMEM((chunks, plane - 1, share, LANES), f32),
-            pltpu.VMEM((chunks, CLUSTERS, share, LANES), f32),
-            pltpu.VMEM((chunks, nb - 1, share, LANES), f32),
-            pltpu.VMEM((chunks, CLUSTERS, share, LANES), f32),
-            pltpu.VMEM((chunks, plane - 1, share, LANES), f32),
+            pltpu.VMEM((chunks, plane - 1, share, WIDE), f32),
+            pltpu.VMEM((chunks, CLUSTERS, share, WIDE), f32),
+            pltpu.VMEM((chunks, nb - 1, share, WIDE), f32),
+            pltpu.VMEM((chunks, CLUSTERS, share, WIDE), f32),
+            pltpu.VMEM((chunks, plane - 1, share, WIDE), f32),
             dma((blocks + 4,)),
             dma, dma, dma, dma,
             *[dma((chunks,)) for _ in range(8)],

time: 44.5 us -> 43.8 us (0.984)
  Pallas kernels: 42.3 us -> 41.5 us
    pallas_call x1, Pallas kernels: 42.3 us -> 41.5 us  [on_device(): pl.pallas_call(functools.partial(kernel, sizes), out_shape=jax.ShapeDtype...]
where the time goes in v5:
time: 43.8 us; the launch traced here: 43.7 us
  Pallas kernels  41.5 us (95%)
  between operations  1.31 us (3%)
  local copies, waits for them, and re-layouts  0.87 us (2%)
    pallas_call x1, Pallas kernels, on_device(): pl.pallas_call(functools.partial(kernel, sizes), out_shape=jax.ShapeDtype...  41.5 us

profile of v5, /device:TPU:1, one launch (start us, length us, event | category | flops | bytes accessed | tf_op | source)
XLA Modules:
  0.0 43.7 jit_solution(4323905981937108886)
XLA Ops:
  1.3 0.1 iota.7.mine
  1.4 41.5 %shard_map.73 = f32[512,256]{1,0:T(8,128)S(1)} custom-call(bf16[1,2048,1024]{2,1,0:T(8,128)(2,1)} %features.1, bf16[1,2048,256]{2,1,0:T(8,128)(2,1)} %targets.1, bf16[1,1024,512]{2,1,0:T(8,128)(2,1)} %lower.1, f32[1,512,256]{2,1,0:T(8,128)} %head.1, s32[1,2,1024]{2,1,0:T(2,128)} %rows.1, f32[8,128]{1,0:T(8,128)S(1)} %iota.7.mine), custom_call_target="tpu_custom_call" | custom-call | tf_op jit(solution)/shard_map/pallas_call | solution.py:283
  42.9 0.8 %copy.11 = f32[1,512,256]{2,1,0:T(8,128)} copy(f32[1,512,256]{2,1,0:T(8,128)S(1)} %bitcast.4) | data formatting | bytes 1048576
  (1 shorter events, 0.0 us)

commit v6 on v5

--- a/solution.py
+++ b/solution.py
@@ -249,9 +249,6 @@
     scale = 1.0 / (LR * (part[...] + jnp.sum(parts[...], axis=0)))
     for h in range(chunks):
         stage3(h, scale)
-    for h in range(chunks):
-        done(got1.at[h], recv4.at[h])
-
     done(meta, meta_send)
     done(parts, part_send)
     for h in range(chunks):
@@ -259,6 +256,9 @@
         done(got2.at[h], send2.at[h])
         done(got2.at[h], send3.at[h])
         done(got1.at[h], send4.at[h])
+
+    for h in range(chunks):
+        done(got1.at[h], recv4.at[h])
 
 
 def on_device(sizes, features, targets, lower_weight, head_weight, batch_rows, sample_counts, cluster_ids):

time: 43.8 us -> 43.8 us (level)
  no operation moved by 1% of the time
where the time goes in v6:
time: 43.8 us; the launch traced here: 43.7 us
  Pallas kernels  41.5 us (95%)
  between operations  1.31 us (3%)
  local copies, waits for them, and re-layouts  0.87 us (2%)
    pallas_call x1, Pallas kernels, on_device(): pl.pallas_call(functools.partial(kernel, sizes), out_shape=jax.ShapeDtype...  41.5 us

profile of v6, /device:TPU:1, one launch (start us, length us, event | category | flops | bytes accessed | tf_op | source)
XLA Modules:
  0.0 43.7 jit_solution(8614277981824270716)
XLA Ops:
  1.3 0.1 iota.7.mine
  1.4 41.5 %shard_map.73 = f32[512,256]{1,0:T(8,128)S(1)} custom-call(bf16[1,2048,1024]{2,1,0:T(8,128)(2,1)} %features.1, bf16[1,2048,256]{2,1,0:T(8,128)(2,1)} %targets.1, bf16[1,1024,512]{2,1,0:T(8,128)(2,1)} %lower.1, f32[1,512,256]{2,1,0:T(8,128)} %head.1, s32[1,2,1024]{2,1,0:T(2,128)} %rows.1, f32[8,128]{1,0:T(8,128)S(1)} %iota.7.mine), custom_call_target="tpu_custom_call" | custom-call | tf_op jit(solution)/shard_map/pallas_call | solution.py:283
  42.9 0.8 %copy.11 = f32[1,512,256]{2,1,0:T(8,128)} copy(f32[1,512,256]{2,1,0:T(8,128)S(1)} %bitcast.4) | data formatting | bytes 1048576
  (1 shorter events, 0.0 us)
